TPU v7x, 8 devices: a whole 2x2x1 slice. The times are simulated.
8 devices in a mesh: fsdp: 8 (over z, y, x, core).
Axes of the slice: x: 2, y: 2, z: 1, core: 2. Of those that a mesh axis runs over, the one named last changes fastest.
Arguments:
- w_up: bfloat16 [1, 2048, 5632], P(None, 'fsdp')
- w_down: bfloat16 [1, 5632, 2048], P(None, 'fsdp')
- tokens_in: bfloat16 [3, 4096, 2048], P(None, 'fsdp')
- cotangent: bfloat16 [3, 4096, 2048], P(None, 'fsdp')
Outputs:
- output 1: bfloat16 [3, 4096, 2048], P(None, 'fsdp')
- output 2: float32 [1, 2048, 5632], P(None, 'fsdp')
- output 3: float32 [1, 5632, 2048], P(None, 'fsdp')
All inputs are finite; a program needn't handle non-finite values.
Results may differ from a plain program's by a relative error of at most 0.001.
Values are sent between devices in bfloat16 or wider.
A program may use at most 1 GiB of HBM per device.

v0:
```python
import jax
import jax.numpy as jnp
from jax import lax
from jax.sharding import PartitionSpec as P


def gelu_fn(pre_act):
    return jax.nn.gelu(pre_act, approximate=True)


def gather_layer(up_shard, down_shard):
    full_up = lax.all_gather(up_shard, 'fsdp', axis=0, tiled=True)
    full_down = lax.all_gather(down_shard, 'fsdp', axis=0, tiled=True)
    return full_up, full_down


def solution(mesh):
    row_spec = P(None, 'fsdp', None)

    def per_device(w_up, w_down, tokens_in, cotangent):
        n_layers = w_up.shape[0]

        def micro_step(acc_pair, micro_in):
            rows_in, cot_rows = micro_in
            saved_rows = []
            rows_cur = rows_in
            for layer_idx in range(n_layers):
                full_up, full_down = gather_layer(w_up[layer_idx], w_down[layer_idx])
                saved_rows.append(rows_cur)
                pre_act = jnp.dot(rows_cur, full_up, preferred_element_type=jnp.float32).astype(jnp.bfloat16)
                hidden = gelu_fn(pre_act.astype(jnp.float32)).astype(jnp.bfloat16)
                summed = rows_cur.astype(jnp.float32) + jnp.dot(hidden, full_down, preferred_element_type=jnp.float32)
                rows_cur = summed.astype(jnp.bfloat16)
            acc_up = list(acc_pair[0])
            acc_down = list(acc_pair[1])
            grad_rows = cot_rows
            for layer_idx in reversed(range(n_layers)):
                full_up, full_down = gather_layer(w_up[layer_idx], w_down[layer_idx])
                rows_prev = saved_rows[layer_idx]
                pre_f32 = jnp.dot(rows_prev, full_up, preferred_element_type=jnp.float32).astype(jnp.bfloat16).astype(jnp.float32)
                hidden_f32, pull_back = jax.vjp(gelu_fn, pre_f32)
                hidden = hidden_f32.astype(jnp.bfloat16)
                part_down = jnp.einsum('tf,td->fd', hidden, grad_rows, preferred_element_type=jnp.float32)
                grad_hid = jnp.einsum('td,fd->tf', grad_rows, full_down, preferred_element_type=jnp.float32)
                grad_pre = pull_back(grad_hid)[0].astype(jnp.bfloat16)
                part_up = jnp.einsum('td,tf->df', rows_prev, grad_pre, preferred_element_type=jnp.float32)
                if layer_idx > 0:
                    grad_prev = grad_rows.astype(jnp.float32) + jnp.einsum('tf,df->td', grad_pre, full_up, preferred_element_type=jnp.float32)
                    grad_rows = grad_prev.astype(jnp.bfloat16)
                acc_down[layer_idx] = acc_down[layer_idx] + lax.psum_scatter(part_down, 'fsdp', scatter_dimension=0, tiled=True)
                acc_up[layer_idx] = acc_up[layer_idx] + lax.psum_scatter(part_up, 'fsdp', scatter_dimension=0, tiled=True)
            return (tuple(acc_up), tuple(acc_down)), rows_cur

        init_up = tuple(jnp.zeros(w_up.shape[1:], jnp.float32) for _ in range(n_layers))
        init_down = tuple(jnp.zeros(w_down.shape[1:], jnp.float32) for _ in range(n_layers))
        acc_pair, tokens_out = lax.scan(micro_step, (init_up, init_down), (tokens_in, cotangent))
        return tokens_out, jnp.stack(acc_pair[0]), jnp.stack(acc_pair[1])

    return jax.shard_map(per_device, mesh=mesh, in_specs=(row_spec, row_spec, row_spec, row_spec), out_specs=(row_spec, row_spec, row_spec), check_vma=False)
```

profile of v0, /device:TPU:0, one launch (start us, length us, event | category | flops | bytes accessed | tf_op | source)
XLA Modules:
  0.0 2376.2 jit_solution(16706842401957830895)
XLA Ops:
  7.2 2362.2 %while.17 = (s32[]{:T(128)}, f32[256,5632]{1,0:T(8,128)}, f32[704,2048]{1,0:T(8,128)}, bf16[3,512,2048]{2,1,0:T(8,128)(2,1)}, bf16[3,512,2048]{2,1,0:T(8,128)(2,...) while((s32[]{:T(128)}, f32[256,5632]{1,0:T(8,128)}, ...), condition=%wide.region_3.4_spmd.clone, body=%wide.region_0.3_spmd.clone.sunk | while | flops 59185823744 | bytes 698877184 | solution.py:56
  8.7 114.7 %all-gather.11.cloned.1.call-done = bf16[1,2048,5632]{2,1,0:T(8,128)(2,1)} async-done(((bf16[1,256,5632]{2,1,0:T(8,128)(2,1)}), bf16[1,2048,5632]{2,1,0:T(8,128)(2,1)}) %all-gather.11.cloned.1.call-update) | async-done | bytes 23068688 | tf_op jit(solution)/shard_map/while/body/eval_jaxpr/all_gather | solution.py:12
  123.4 18.9 fusion.77
  142.3 93.7 %all-gather.13.cloned.1.call-done = bf16[1,5632,2048]{2,1,0:T(8,128)(2,1)} async-done(((bf16[1,704,2048]{2,1,0:T(8,128)(2,1)}), bf16[1,5632,2048]{2,1,0:T(8,128)(2,1)}) %all-gather.13.cloned.1.call-update) | async-done | bytes 23068688 | tf_op jit(solution)/shard_map/while/body/eval_jaxpr/all_gather | solution.py:13
  236.0 38.7 %fusion.78 = f32[2048,5632]{1,0:T(8,128)} fusion(bf16[3,512,2048]{2,1,0:T(8,128)(2,1)} %get-tuple-element.225, s32[]{:T(128)S(6)} %copy.12, bf16[512,5632]{1,0:T(8,128)(2,1)} %fusion.77, bf16[1,5632,2048]{2,1,0:T(8,128)(2,1)} %all-gather.13.cloned.1.call-done, bf16[3,512,2048]{2,1,0:T(8,128)(2,1)} %get-tuple-element.226), kind=kOutput, calls=%fused_computation.30.clone.1 | convolution fusion | flops 23682875392 | bytes 79168512 | tf_op jit(solution)/shard_map/while/body/eval_jaxpr/td,tf->df/dot_general | solution.py:46
  274.8 28.0 %fusion.79 = f32[5632,2048]{1,0:T(8,128)} fusion(bf16[3,512,2048]{2,1,0:T(8,128)(2,1)} %get-tuple-element.226, s32[]{:T(128)S(6)} %copy.12, bf16[512,5632]{1,0:T(8,128)(2,1)} %fusion.77), kind=kOutput, calls=%fused_computation.27.clone.1 | convolution fusion | flops 11839995904 | bytes 54001668 | tf_op jit(solution)/shard_map/while/body/eval_jaxpr/tf,td->fd/dot_general | solution.py:43
  302.8 22.0 fusion.80
  324.8 205.2 %reduce-scatter.3.cloned.1.call-done = f32[256,5632]{1,0:T(8,128)} async-done(((f32[2048,5632]{1,0:T(8,128)}), f32[256,5632]{1,0:T(8,128)}) %reduce-scatter.3.cloned.1.call-update) | async-done | bytes 5767184 | tf_op jit(solution)/shard_map/while/body/eval_jaxpr/reduce_scatter | solution.py:51
  530.0 6.0 select_add_fusion.4
  535.9 252.6 %reduce-scatter.5.cloned.1.call-done = f32[704,2048]{1,0:T(8,128)} async-done(((f32[5632,2048]{1,0:T(8,128)}), f32[704,2048]{1,0:T(8,128)}) %reduce-scatter.5.cloned.1.call-update) | async-done | bytes 5767184 | tf_op jit(solution)/shard_map/while/body/eval_jaxpr/reduce_scatter | solution.py:50
  788.5 7.0 select_add_fusion.5
  796.7 111.9 %all-gather.11.cloned.1.call-done = bf16[1,2048,5632]{2,1,0:T(8,128)(2,1)} async-done(((bf16[1,256,5632]{2,1,0:T(8,128)(2,1)}), bf16[1,2048,5632]{2,1,0:T(8,128)(2,1)}) %all-gather.11.cloned.1.call-update) | async-done | bytes 23068688 | tf_op jit(solution)/shard_map/while/body/eval_jaxpr/all_gather | solution.py:12
  908.6 18.8 fusion.77
  927.4 93.6 %all-gather.13.cloned.1.call-done = bf16[1,5632,2048]{2,1,0:T(8,128)(2,1)} async-done(((bf16[1,704,2048]{2,1,0:T(8,128)(2,1)}), bf16[1,5632,2048]{2,1,0:T(8,128)(2,1)}) %all-gather.13.cloned.1.call-update) | async-done | bytes 23068688 | tf_op jit(solution)/shard_map/while/body/eval_jaxpr/all_gather | solution.py:13
  1021.0 38.7 %fusion.78 = f32[2048,5632]{1,0:T(8,128)} fusion(bf16[3,512,2048]{2,1,0:T(8,128)(2,1)} %get-tuple-element.225, s32[]{:T(128)S(6)} %copy.12, bf16[512,5632]{1,0:T(8,128)(2,1)} %fusion.77, bf16[1,5632,2048]{2,1,0:T(8,128)(2,1)} %all-gather.13.cloned.1.call-done, bf16[3,512,2048]{2,1,0:T(8,128)(2,1)} %get-tuple-element.226), kind=kOutput, calls=%fused_computation.30.clone.1 | convolution fusion | flops 23682875392 | bytes 79168512 | tf_op jit(solution)/shard_map/while/body/eval_jaxpr/td,tf->df/dot_general | solution.py:46
  1059.8 28.0 %fusion.79 = f32[5632,2048]{1,0:T(8,128)} fusion(bf16[3,512,2048]{2,1,0:T(8,128)(2,1)} %get-tuple-element.226, s32[]{:T(128)S(6)} %copy.12, bf16[512,5632]{1,0:T(8,128)(2,1)} %fusion.77), kind=kOutput, calls=%fused_computation.27.clone.1 | convolution fusion | flops 11839995904 | bytes 54001668 | tf_op jit(solution)/shard_map/while/body/eval_jaxpr/tf,td->fd/dot_general | solution.py:43
  1087.8 22.0 fusion.80
  1109.8 205.2 %reduce-scatter.3.cloned.1.call-done = f32[256,5632]{1,0:T(8,128)} async-done(((f32[2048,5632]{1,0:T(8,128)}), f32[256,5632]{1,0:T(8,128)}) %reduce-scatter.3.cloned.1.call-update) | async-done | bytes 5767184 | tf_op jit(solution)/shard_map/while/body/eval_jaxpr/reduce_scatter | solution.py:51
  1315.0 7.7 select_add_fusion.4
  1322.6 251.0 %reduce-scatter.5.cloned.1.call-done = f32[704,2048]{1,0:T(8,128)} async-done(((f32[5632,2048]{1,0:T(8,128)}), f32[704,2048]{1,0:T(8,128)}) %reduce-scatter.5.cloned.1.call-update) | async-done | bytes 5767184 | tf_op jit(solution)/shard_map/while/body/eval_jaxpr/reduce_scatter | solution.py:50
  1573.7 8.7 select_add_fusion.5
  1582.3 0.7 all-gather.11.cloned.1.call-update
  1583.7 112.0 %all-gather.11.cloned.1.call-done = bf16[1,2048,5632]{2,1,0:T(8,128)(2,1)} async-done(((bf16[1,256,5632]{2,1,0:T(8,128)(2,1)}), bf16[1,2048,5632]{2,1,0:T(8,128)(2,1)}) %all-gather.11.cloned.1.call-update) | async-done | bytes 23068688 | tf_op jit(solution)/shard_map/while/body/eval_jaxpr/all_gather | solution.py:12
  1695.7 18.7 fusion.77
  1714.5 93.7 %all-gather.13.cloned.1.call-done = bf16[1,5632,2048]{2,1,0:T(8,128)(2,1)} async-done(((bf16[1,704,2048]{2,1,0:T(8,128)(2,1)}), bf16[1,5632,2048]{2,1,0:T(8,128)(2,1)}) %all-gather.13.cloned.1.call-update) | async-done | bytes 23068688 | tf_op jit(solution)/shard_map/while/body/eval_jaxpr/all_gather | solution.py:13
  1808.2 38.7 %fusion.78 = f32[2048,5632]{1,0:T(8,128)} fusion(bf16[3,512,2048]{2,1,0:T(8,128)(2,1)} %get-tuple-element.225, s32[]{:T(128)S(6)} %copy.12, bf16[512,5632]{1,0:T(8,128)(2,1)} %fusion.77, bf16[1,5632,2048]{2,1,0:T(8,128)(2,1)} %all-gather.13.cloned.1.call-done, bf16[3,512,2048]{2,1,0:T(8,128)(2,1)} %get-tuple-element.226), kind=kOutput, calls=%fused_computation.30.clone.1 | convolution fusion | flops 23682875392 | bytes 79168512 | tf_op jit(solution)/shard_map/while/body/eval_jaxpr/td,tf->df/dot_general | solution.py:46
  1846.9 28.0 %fusion.79 = f32[5632,2048]{1,0:T(8,128)} fusion(bf16[3,512,2048]{2,1,0:T(8,128)(2,1)} %get-tuple-element.226, s32[]{:T(128)S(6)} %copy.12, bf16[512,5632]{1,0:T(8,128)(2,1)} %fusion.77), kind=kOutput, calls=%fused_computation.27.clone.1 | convolution fusion | flops 11839995904 | bytes 54001668 | tf_op jit(solution)/shard_map/while/body/eval_jaxpr/tf,td->fd/dot_general | solution.py:43
  1874.9 22.0 fusion.80
  1896.9 205.2 %reduce-scatter.3.cloned.1.call-done = f32[256,5632]{1,0:T(8,128)} async-done(((f32[2048,5632]{1,0:T(8,128)}), f32[256,5632]{1,0:T(8,128)}) %reduce-scatter.3.cloned.1.call-update) | async-done | bytes 5767184 | tf_op jit(solution)/shard_map/while/body/eval_jaxpr/reduce_scatter | solution.py:51
  2102.1 7.7 select_add_fusion.4
  2109.8 250.9 %reduce-scatter.5.cloned.1.call-done = f32[704,2048]{1,0:T(8,128)} async-done(((f32[5632,2048]{1,0:T(8,128)}), f32[704,2048]{1,0:T(8,128)}) %reduce-scatter.5.cloned.1.call-update) | async-done | bytes 5767184 | tf_op jit(solution)/shard_map/while/body/eval_jaxpr/reduce_scatter | solution.py:50
  2360.7 8.7 select_add_fusion.5
  (26 shorter events, 3.5 us)
Async XLA Ops:
  7.2 116.2 %all-gather.11.cloned.1.call-start = ((), (), s32[]{:S(2)}) async-start(), calls=%async_computation.2 | async-start | bytes 25952256 | tf_op jit(solution)/shard_map/while/body/eval_jaxpr/all_gather | solution.py:12
  7.9 228.1 %all-gather.13.cloned.1.call-start = ((), (), s32[]{:S(2)}) async-start(), calls=%async_computation.3 | async-start | bytes 25952256 | tf_op jit(solution)/shard_map/while/body/eval_jaxpr/all_gather | solution.py:13
  8.7 521.3 %reduce-scatter.3.cloned.1.call-start = ((), (), s32[]{:S(2)}) async-start(), calls=%async_computation.4 | async-start | bytes 51904512 | tf_op jit(solution)/shard_map/while/body/eval_jaxpr/reduce_scatter | solution.py:51
  274.7 513.8 %reduce-scatter.5.cloned.1.call-start = ((), (), s32[]{:S(2)}) async-start(), calls=%async_computation.5 | async-start | bytes 51904512 | tf_op jit(solution)/shard_map/while/body/eval_jaxpr/reduce_scatter | solution.py:50
  795.5 113.1 %all-gather.11.cloned.1.call-start = ((), (), s32[]{:S(2)}) async-start(), calls=%async_computation.2 | async-start | bytes 25952256 | tf_op jit(solution)/shard_map/while/body/eval_jaxpr/all_gather | solution.py:12
  796.1 225.0 %all-gather.13.cloned.1.call-start = ((), (), s32[]{:S(2)}) async-start(), calls=%async_computation.3 | async-start | bytes 25952256 | tf_op jit(solution)/shard_map/while/body/eval_jaxpr/all_gather | solution.py:13
  796.7 518.3 %reduce-scatter.3.cloned.1.call-start = ((), (), s32[]{:S(2)}) async-start(), calls=%async_computation.4 | async-start | bytes 51904512 | tf_op jit(solution)/shard_map/while/body/eval_jaxpr/reduce_scatter | solution.py:51
  1059.7 513.9 %reduce-scatter.5.cloned.1.call-start = ((), (), s32[]{:S(2)}) async-start(), calls=%async_computation.5 | async-start | bytes 51904512 | tf_op jit(solution)/shard_map/while/body/eval_jaxpr/reduce_scatter | solution.py:50
  1582.3 113.4 %all-gather.11.cloned.1.call-start = ((), (), s32[]{:S(2)}) async-start(), calls=%async_computation.2 | async-start | bytes 25952256 | tf_op jit(solution)/shard_map/while/body/eval_jaxpr/all_gather | solution.py:12
  1583.1 225.1 %all-gather.13.cloned.1.call-start = ((), (), s32[]{:S(2)}) async-start(), calls=%async_computation.3 | async-start | bytes 25952256 | tf_op jit(solution)/shard_map/while/body/eval_jaxpr/all_gather | solution.py:13
  1583.7 518.5 %reduce-scatter.3.cloned.1.call-start = ((), (), s32[]{:S(2)}) async-start(), calls=%async_computation.4 | async-start | bytes 51904512 | tf_op jit(solution)/shard_map/while/body/eval_jaxpr/reduce_scatter | solution.py:51
  1846.9 513.8 %reduce-scatter.5.cloned.1.call-start = ((), (), s32[]{:S(2)}) async-start(), calls=%async_computation.5 | async-start | bytes 51904512 | tf_op jit(solution)/shard_map/while/body/eval_jaxpr/reduce_scatter | solution.py:50
Sparse Core Ops, SparseCore 0:
  9.8 113.5 all-gather.10
  125.3 110.7 all-gather.12
  274.8 255.0 reduce-scatter.2
  533.4 255.0 reduce-scatter.4
  797.8 110.7 all-gather.10
  910.3 110.7 all-gather.12
  1059.8 255.0 reduce-scatter.2
  1318.5 255.0 reduce-scatter.4
  1585.0 110.7 all-gather.10
  1697.4 110.7 all-gather.12
  1847.0 255.0 reduce-scatter.2
  2105.5 255.0 reduce-scatter.4
where the time goes:
time: 2380 us
  waiting for transfers between devices  1990 us (84%)
  matrix products  322 us (14%)
  other arithmetic  45.6 us (2%)
    reduce_scatter x3, waiting for transfers between devices, micro_step(): lax.psum_scatter(part_down, 'fsdp', scatter_dimension=0, tiled=True)  755 us
    reduce_scatter x3, waiting for transfers between devices, micro_step(): lax.psum_scatter(part_up, 'fsdp', scatter_dimension=0, tiled=True)  616 us
    all_gather x3, waiting for transfers between devices, gather_layer(): full_up = lax.all_gather(up_shard, 'fsdp', axis=0, tiled=True)  339 us
    all_gather x3, waiting for transfers between devices, gather_layer(): full_down = lax.all_gather(down_shard, 'fsdp', axis=0, tiled=True)  281 us
    dot_general x3, matrix products, micro_step(): jnp.einsum('td,tf->df', rows_prev, grad_pre, preferred_element_type=jnp.f...  116 us
    dot_general x3, matrix products, micro_step(): jnp.einsum('tf,td->fd', hidden, grad_rows, preferred_element_type=jnp.flo...  84 us
    dot_general x3, matrix products, micro_step(): jnp.dot(hidden, full_down, preferred_element_type=jnp.float32)  66 us
    dot_general x3, matrix products, micro_step(): jnp.dot(rows_prev, full_up, preferred_element_type=jnp.float32)  56.4 us
  transfers between devices with their start and end apart: 12, of which 12 were waited for; matrix products, arithmetic and copies ran while one was open for 10% of the time, Pallas kernels for 0%

commit v1 on v0

v1 whole, which is shorter than its diff:
```python
import functools
import math

import jax
import jax.numpy as jnp
from jax import lax
from jax.experimental import pallas as pl
from jax.experimental.pallas import tpu as pltpu
from jax.sharding import PartitionSpec as P

F32 = jnp.float32
BF16 = jnp.bfloat16
N_CHUNK = 11
LAG_T = 4
LAG_Z = 8
N_K = 8
N_H = 3
N_T = 4
Y_STEP = 5
GELU_C = math.sqrt(2.0 / math.pi)
NN = (((1,), (0,)), ((), ()))
NT_DIMS = (((1,), (1,)), ((), ()))
TN_DIMS = (((0,), (0,)), ((), ()))


def matmul(a, b, dims=NN):
    return lax.dot_general(a, b, dims, preferred_element_type=F32)


def aligned(start, size):
    return pl.ds(pl.multiple_of(start, size), size)


def kernel(sizes, w1, w2, x, g, y, gup, gdown, w1f, w2f, a_h, h_h, ht_h, r_s, r_h, r_t,
           x_v, g_v, y_acc, w1_ss, w1_rs, w2_ss, w2_rs, c_rs, s_ss, h_ss, t_ss, loc, out_sem, io_sem, ld_sem):
    tokens, d_model, d_ff = sizes
    fc = d_ff // N_CHUNK
    d_blk = d_model // 8
    f_blk = d_ff // 8
    r2 = f_blk // N_CHUNK
    n_tile = d_model // fc
    n_q = 2 * N_CHUNK
    row_t = tokens // 3
    n_row = 3
    pieces = ((0, 2), (2, 3), (5, 3), (8, 3))
    n_piece = 4
    p_rows = f_blk // n_piece

    me = lax.axis_index('fsdp')
    core = me % 2
    cx = (me // 2) % 2
    cy = me // 4
    chip = me // 2

    def dev(flip_y, flip_x, flip_c):
        yy = 1 - cy if flip_y else cy
        xx = 1 - cx if flip_x else cx
        cc = 1 - core if flip_c else core
        return 4 * yy + 2 * xx + cc

    sib, xn, yn = dev(0, 0, 1), dev(0, 1, 0), dev(1, 0, 0)
    diag = dev(1, 1, 0)
    origins = (xn, yn, diag, sib, dev(0, 1, 1), dev(1, 0, 1), dev(1, 1, 1))

    def remote(src, dst, ssem, rsem, to):
        return pltpu.make_async_remote_copy(src_ref=src, dst_ref=dst, send_sem=ssem, recv_sem=rsem,
                                            device_id=(to,), device_id_type=pl.DeviceIdType.MESH)

    barrier = pltpu.get_barrier_semaphore()
    for other in (sib, xn, yn):
        pl.semaphore_signal(barrier, inc=1, device_id=(other,), device_id_type=pl.DeviceIdType.MESH)
    pl.semaphore_wait(barrier, 3)

    def w1_cols(p):
        return pl.ds(pieces[p][0] * fc, pieces[p][1] * fc)

    def w1_copy(kind, p, origin, to, own=False):
        src = w1.at[:, w1_cols(p)] if own else w1f.at[origin, :, w1_cols(p)]
        return remote(src, w1f.at[origin, :, w1_cols(p)], w1_ss.at[kind, p], w1_rs.at[kind, p], to)

    def w2_copy(kind, p, origin, to, own=False):
        rows = aligned(p * p_rows, p_rows)
        full = aligned(origin * f_blk + p * p_rows, p_rows)
        src = w2.at[rows, :] if own else w2f.at[full, :]
        return remote(src, w2f.at[full, :], w2_ss.at[kind, p], w2_rs.at[kind, p], to)

    def w1_recv(kind, p):
        w1_copy(kind, p, origins[kind], me).wait_recv()

    def w2_recv(kind, p):
        w2_copy(kind, p, origins[kind], me).wait_recv()

    def own_w1(p):
        w1_copy(0, p, me, xn, own=True).start()
        w1_copy(1, p, me, yn, own=True).start()

    def own_w2(p):
        w2_copy(0, p, me, xn, own=True).start()
        w2_copy(1, p, me, yn, own=True).start()

    own_w1(0)
    own_w1(1)
    for p in range(n_piece):
        w1_copy(3, p, me, sib, own=True).start()
    for p in range(n_piece):
        w2_copy(3, p, me, sib, own=True).start()

    load_x = pltpu.make_async_copy(x, x_v, io_sem.at[0])
    load_g = pltpu.make_async_copy(g, g_v, io_sem.at[1])
    load_x.start()
    load_g.start()

    def stage_own(buf1, buf2):
        in1 = pltpu.make_async_copy(w1, buf1, io_sem.at[2])
        in2 = pltpu.make_async_copy(w2, buf2, io_sem.at[3])
        in1.start()
        in2.start()
        in1.wait()
        out1 = pltpu.make_async_copy(buf1, w1f.at[me], io_sem.at[2])
        out1.start()
        in2.wait()
        out2 = pltpu.make_async_copy(buf2, w2f.at[aligned(me * f_blk, f_blk), :], io_sem.at[3])
        out2.start()
        out1.wait()
        out2.wait()

    pl.run_scoped(stage_own, pltpu.VMEM((d_blk, d_ff), BF16), pltpu.VMEM((f_blk, d_model), BF16))
    load_x.wait()
    load_g.wait()

    def init_rows(r, _):
        rows = aligned(r * row_t, row_t)
        y_acc[rows, :] = x_v[rows, :].astype(F32)
        return 0

    lax.fori_loop(0, n_row, init_rows, 0)

    def pass_one(wb, ab, hb, htb):
        def w1_load(k, slot):
            return pltpu.make_async_copy(w1f.at[:, :, aligned(k * fc, fc)], wb.at[slot], ld_sem.at[slot])

        def stores(k, slot):
            cols = aligned(k * fc, fc)
            return (pltpu.make_async_copy(ab.at[slot], a_h.at[:, cols], loc.at[0, slot]),
                    pltpu.make_async_copy(hb.at[slot], h_h.at[:, cols], loc.at[1, slot]),
                    pltpu.make_async_copy(htb.at[slot], ht_h.at[cols, :], loc.at[2, slot]))

        def compute(p):
            for kind in (3, 4, 5, 6):
                w1_recv(kind, p)
            first, count = pieces[p]
            w1_load(first, first % 2).start()

            def chunk(k, _):
                slot = k % 2
                w1_load(k, slot).wait()

                @pl.when(k + 1 < first + count)
                def _():
                    w1_load(k + 1, 1 - slot).start()

                @pl.when(k >= 2)
                def _():
                    for cp in stores(k - 2, slot):
                        cp.wait()

                def rows_loop(r, _):
                    rows = aligned(r * row_t, row_t)
                    acc = matmul(x_v[rows, :], wb[slot].reshape(d_model, fc)).astype(BF16)
                    ab[slot, rows, :] = acc
                    u = acc.astype(F32)
                    t = jnp.tanh(GELU_C * (u + 0.044715 * (u * u * u)))
                    hid = (u * (0.5 * (1.0 + t))).astype(BF16)
                    hb[slot, rows, :] = hid
                    htb[slot, :, rows] = hid.T
                    return 0

                lax.fori_loop(0, n_row, rows_loop, 0)
                for cp in stores(k, slot):
                    cp.start()
                return 0

            lax.fori_loop(first, first + count, chunk, 0)

        def diag_forward(p):
            w1_recv(2, p)
            w1_copy(6, p, diag, sib).start()

        for p in range(n_piece):
            w1_recv(0, p)
            w1_copy(4, p, xn, sib).start()
            if p % 2:
                w1_copy(2, p, xn, yn).start()
            w1_recv(1, p)
            w1_copy(5, p, yn, sib).start()
            if not p % 2:
                w1_copy(2, p, yn, xn).start()
            if p + 2 < n_piece:
                own_w1(p + 2)
            else:
                own_w2(p + 2 - n_piece)
            if p >= 1:
                diag_forward(p - 1)
            if p >= 2:
                compute(p - 2)
        own_w2(2)
        own_w2(3)
        diag_forward(n_piece - 1)
        compute(n_piece - 2)
        compute(n_piece - 1)
        for k in (N_CHUNK - 2, N_CHUNK - 1):
            for cp in stores(k, k % 2):
                cp.wait()

    pl.run_scoped(pass_one, pltpu.VMEM((2, 8, d_blk, fc), BF16), pltpu.VMEM((2, tokens, fc), BF16),
                  pltpu.VMEM((2, tokens, fc), BF16), pltpu.VMEM((2, fc, tokens), BF16))

    def pick(par, even, odd):
        return even * (1 - par) + odd * par

    def first_dev(q):
        return pick(q % 2, xn, yn)

    def second_dev(q):
        return pick(q % 2, yn, xn)

    def chips_of(q):
        return (first_dev(q) // 2, 3 - chip, chip, second_dev(q) // 2)

    def main(s_b, m_b, k_b, h_b, t_b, z_b, st_s, st_h, st_t, q_v, lhs, w2e, a_v, w2y, hy):

        def send_s(q):
            return remote(s_b.at[q % 2], r_s.at[q], s_ss.at[q % 2], c_rs.at[0, q], sib)

        def send_h(q):
            return remote(h_b.at[q % N_H], r_h.at[q], h_ss.at[q % N_H], c_rs.at[1, q], first_dev(q))

        def send_t(q):
            return remote(t_b.at[q % N_T], r_t.at[q], t_ss.at[q % N_T], c_rs.at[2, q], second_dev(q))

        def lhs_loads(q):
            cps = []
            for b, mb in enumerate(chips_of(q)):
                for j, cc in enumerate((1 - core, core)):
                    rows = aligned(f_blk * (2 * mb + cc) + r2 * q, r2)
                    cps.append(pltpu.make_async_copy(ht_h.at[rows, :], lhs.at[4 * j + b], ld_sem.at[0]))
            return cps

        def lhs_wait():
            pltpu.make_async_copy(lhs, lhs, ld_sem.at[0]).wait()

        def e_loads(k):
            return (pltpu.make_async_copy(w2f.at[aligned(k * fc, fc), :], w2e, ld_sem.at[1]),
                    pltpu.make_async_copy(a_h.at[:, aligned(k * fc, fc)], a_v, ld_sem.at[2]))

        def y_loads(k):
            return (pltpu.make_async_copy(w2f.at[aligned(k * fc, fc), :], w2y, ld_sem.at[3]),
                    pltpu.make_async_copy(h_h.at[:, aligned(k * fc, fc)], hy, ld_sem.at[4]))

        def z_out(q, cond_down):
            slot = q % 2
            if cond_down:
                return [pltpu.make_async_copy(z_b.at[slot, n * r2:(n + 1) * r2, :],
                                              gdown.at[aligned(q * r2, r2), n * fc:(n + 1) * fc], out_sem.at[slot])
                        for n in range(n_tile)]
            return [pltpu.make_async_copy(z_b.at[slot], gup.at[:, aligned((q - N_CHUNK) * fc, fc)], out_sem.at[slot])]

        def z_wait(q):
            pltpu.make_async_copy(z_b.at[q % 2], gup.at[:, pl.ds(0, fc)], out_sem.at[q % 2]).wait()

        for cp in lhs_loads(0):
            cp.start()

        def step(s, _):
            @pl.when(s < n_piece)
            def _():
                w2_recv(0, s)
                w2_copy(4, s, xn, sib).start()
                w2_recv(1, s)
                w2_copy(5, s, yn, sib).start()
                w2_copy(2, s, pick(s % 2, yn, xn), pick(s % 2, xn, yn)).start()

            @pl.when((s >= 1) & (s < n_piece + 1))
            def _():
                w2_recv(2, s - 1)
                w2_copy(6, s - 1, diag, sib).start()

            @pl.when(s == Y_STEP)
            def _():
                for p in range(n_piece):
                    for kind in (3, 4, 5, 6):
                        w2_recv(kind, p)
                for cp in y_loads(0):
                    cp.start()
                for cp in e_loads(0):
                    cp.start()

            @pl.when((s >= 1) & (s - 1 < n_q))
            def _():
                q = s - 1
                send_s(q).wait_recv()
                ld = pltpu.make_async_copy(r_s.at[q], st_s, io_sem.at[0])
                ld.start()

                @pl.when(q >= N_H)
                def _():
                    send_h(q - N_H).wait_send()

                ld.wait()
                h_b[q % N_H] = m_b[0:2] + st_s[0:2]
                k_b[q % N_K] = m_b[2:4] + st_s[2:4]
                send_h(q).start()

            @pl.when((s >= LAG_T) & (s - LAG_T < n_q))
            def _():
                q = s - LAG_T
                send_h(q).wait_recv()
                ld = pltpu.make_async_copy(r_h.at[q], st_h, io_sem.at[1])
                ld.start()

                @pl.when(q >= N_T)
                def _():
                    send_t(q - N_T).wait_send()

                ld.wait()
                t_b[q % N_T] = k_b[q % N_K, 1] + st_h[1]
                send_t(q).start()
                k_b[q % N_K, 0] = k_b[q % N_K, 0] + st_h[0]

            @pl.when(s >= LAG_Z)
            def _():
                q = s - LAG_Z
                send_t(q).wait_recv()
                ld = pltpu.make_async_copy(r_t.at[q], st_t, io_sem.at[2])
                ld.start()

                @pl.when(q >= 2)
                def _():
                    z_wait(q - 2)

                ld.wait()
                z_b[q % 2] = k_b[q % N_K, 0] + st_t[...]

                @pl.when(q < N_CHUNK)
                def _():
                    for cp in z_out(q, True):
                        cp.start()

                @pl.when(q >= N_CHUNK)
                def _():
                    for cp in z_out(q, False):
                        cp.start()

            @pl.when((s >= 2) & (s < n_q))
            def _():
                send_s(s - 2).wait_send()

            @pl.when(s < N_CHUNK)
            def _():
                lhs_wait()

                def tile(n, _):
                    cols = aligned(n * fc, fc)
                    res = matmul(lhs[...].reshape(8 * r2, tokens), g_v[:, cols])
                    rows = aligned(n * r2, r2)
                    for b in range(4):
                        s_b[s % 2, b, rows, :] = res[b * r2:(b + 1) * r2]
                        m_b[b, rows, :] = res[(4 + b) * r2:(5 + b) * r2]
                    return 0

                lax.fori_loop(0, n_tile, tile, 0)
                send_s(s).start()

                @pl.when(s + 1 < N_CHUNK)
                def _():
                    for cp in lhs_loads(s + 1):
                        cp.start()

            @pl.when((s >= N_CHUNK) & (s < n_q))
            def _():
                k = s - N_CHUNK
                for cp in e_loads(k):
                    cp.wait()

                def rows_loop(r, _):
                    rows = aligned(r * row_t, row_t)
                    e = matmul(g_v[rows, :], w2e[...], NT_DIMS)
                    u = a_v[rows, :].astype(F32)
                    u2 = u * u
                    t = jnp.tanh(GELU_C * (u + 0.044715 * (u2 * u)))
                    slope = 0.5 * (1.0 + t) + (0.5 * u * (1.0 - t * t)) * GELU_C * (1.0 + 0.134145 * u2)
                    q_v[rows, :] = (e * slope).astype(BF16)
                    return 0

                lax.fori_loop(0, n_row, rows_loop, 0)

                @pl.when(k + 1 < N_CHUNK)
                def _():
                    for cp in e_loads(k + 1):
                        cp.start()

                for b, mb in enumerate(chips_of(s)):
                    for cc, dst in ((1 - core, s_b.at[s % 2]), (core, m_b)):
                        rows = aligned(d_blk * (2 * mb + cc), d_blk)
                        dst[b] = matmul(x_v[:, rows], q_v[...], TN_DIMS)
                send_s(s).start()

            @pl.when((s >= Y_STEP) & (s < Y_STEP + N_CHUNK))
            def _():
                k = s - Y_STEP
                for cp in y_loads(k):
                    cp.wait()

                def rows_loop(r, _):
                    rows = aligned(r * row_t, row_t)
                    y_acc[rows, :] += matmul(hy[rows, :], w2y[...])
                    return 0

                lax.fori_loop(0, n_row, rows_loop, 0)

                @pl.when(k + 1 < N_CHUNK)
                def _():
                    for cp in y_loads(k + 1):
                        cp.start()

            @pl.when(s == Y_STEP + N_CHUNK)
            def _():
                for n in range(n_tile):
                    hy[...] = y_acc[:, n * fc:(n + 1) * fc].astype(BF16)
                    cp = pltpu.make_async_copy(hy, y.at[:, n * fc:(n + 1) * fc], ld_sem.at[4])
                    cp.start()
                    cp.wait()

            return 0

        lax.fori_loop(0, n_q + LAG_Z, step, 0)
        send_s(n_q - 2).wait_send()
        send_s(n_q - 1).wait_send()
        for q in range(n_q - N_H, n_q):
            send_h(q).wait_send()
        for q in range(n_q - N_T, n_q):
            send_t(q).wait_send()
        z_wait(n_q - 2)
        z_wait(n_q - 1)

    blk = (d_blk, fc)
    pl.run_scoped(main, pltpu.VMEM((2, 4) + blk, F32), pltpu.VMEM((4,) + blk, F32), pltpu.VMEM((N_K, 2) + blk, F32),
                  pltpu.VMEM((N_H, 2) + blk, F32), pltpu.VMEM((N_T,) + blk, F32), pltpu.VMEM((2,) + blk, F32),
                  pltpu.VMEM((4,) + blk, F32), pltpu.VMEM((2,) + blk, F32), pltpu.VMEM(blk, F32),
                  pltpu.VMEM((tokens, fc), BF16), pltpu.VMEM((8, r2, tokens), BF16),
                  pltpu.VMEM((fc, d_model), BF16), pltpu.VMEM((tokens, fc), BF16),
                  pltpu.VMEM((fc, d_model), BF16), pltpu.VMEM((tokens, fc), BF16))

    for kind in range(7):
        for p in range(n_piece):
            w1_copy(kind, p, me, sib).wait_send()
            w2_copy(kind, p, me, sib).wait_send()


def fused_step(w1, w2, x, g):
    tokens, d_model = x.shape
    d_ff = w1.shape[1]
    fc = d_ff // N_CHUNK
    d_blk = d_model // 8
    n_q = 2 * N_CHUNK
    shape = jax.ShapeDtypeStruct
    any_spec = pl.BlockSpec(memory_space=pl.ANY)
    dma = pltpu.SemaphoreType.DMA
    out_shape = (
        shape((tokens, d_model), BF16),
        shape((d_blk, d_ff), F32),
        shape((d_ff // 8, d_model), F32),
        shape((8, d_blk, d_ff), BF16),
        shape((d_ff, d_model), BF16),
        shape((tokens, d_ff), BF16),
        shape((tokens, d_ff), BF16),
        shape((d_ff, tokens), BF16),
        shape((n_q, 4, d_blk, fc), F32),
        shape((n_q, 2, d_blk, fc), F32),
        shape((n_q, d_blk, fc), F32),
    )
    outs = pl.pallas_call(
        functools.partial(kernel, (tokens, d_model, d_ff)),
        out_shape=out_shape,
        in_specs=[any_spec] * 4,
        out_specs=tuple([any_spec] * len(out_shape)),
        scratch_shapes=[
            pltpu.VMEM((tokens, d_model), BF16),
            pltpu.VMEM((tokens, d_model), BF16),
            pltpu.VMEM((tokens, d_model), F32),
            dma((7, 4)), dma((7, 4)), dma((7, 4)), dma((7, 4)),
            dma((3, n_q)), dma((2,)), dma((N_H,)), dma((N_T,)),
            dma((3, 2)), dma((2,)), dma((4,)), dma((5,)),
        ],
        compiler_params=pltpu.CompilerParams(collective_id=0, has_side_effects=True, vmem_limit_bytes=67000000),
        name="mlp_step",
    )(w1, w2, x, g)
    return outs[0], outs[1], outs[2]


def solution(mesh):
    row_spec = P(None, 'fsdp', None)

    def per_device(w_up, w_down, tokens_in, cotangent):
        width = tokens_in.shape[-1]
        y, gup, gdown = fused_step(w_up[0], w_down[0], tokens_in.reshape(-1, width), cotangent.reshape(-1, width))
        return y.reshape(tokens_in.shape), gup[None], gdown[None]

    return jax.shard_map(per_device, mesh=mesh, in_specs=(row_spec,) * 4, out_specs=(row_spec,) * 3, check_vma=False)
```

time: 2380 us -> 597 us (0.25)
  waiting for transfers between devices: 1990 us -> 0 us
  Pallas kernels: 0 us -> 580 us
  matrix products: 322 us -> 0 us
  other arithmetic: 45.6 us -> 0 us
    reduce_scatter x6 -> x0, waiting for transfers between devices: 1370 us -> none  [the longest x3 755 us: micro_step(): lax.psum_scatter(part_down, 'fsdp', scatter_dimension=0, tiled=True)]
    all_gather x6 -> x0, waiting for transfers between devices: 620 us -> none  [the longest x3 339 us: gather_layer(): full_up = lax.all_gather(up_shard, 'fsdp', axis=0, tiled=True)]
    pallas_call x0 -> x1, Pallas kernels: none -> 580 us  [fused_step(): pl.pallas_call(functools.partial(kernel, (tokens, d_model, d_ff)), out_sh...]
    dot_general x12 -> x0, matrix products: 322 us -> none  [the longest x3 116 us: micro_step(): jnp.einsum('td,tf->df', rows_prev, grad_pre, preferred_element_type=jnp.f...]
    add x6 -> x0, other arithmetic: 45.6 us -> none  [the longest x3 24.3 us: micro_step(): acc_down[layer_idx]]
  transfers between devices with their start and end apart: 12 -> 0, of which waited for: 12 -> 0; matrix products, arithmetic and copies ran while one was open for 10% -> 0% of each run, Pallas kernels for 0% -> 0%
where the time goes in v1:
time: 597 us; the launch traced here: 595 us
  Pallas kernels  580 us (97%)
  local copies, waits for them, and re-layouts  14 us (2%)
    pallas_call x1, Pallas kernels, fused_step(): pl.pallas_call(functools.partial(kernel, (tokens, d_model, d_ff)), out_sh...  580 us
    unnamed x7, local copies, waits for them, and re-layouts  14 us

profile of v1, /device:TPU:0, one launch (start us, length us, event | category | flops | bytes accessed | tf_op | source)
XLA Modules:
  0.0 594.6 jit_solution(15238467602775659778)
XLA Ops:
  0.6 579.9 %mlp_step.1 = (bf16[1536,2048]{1,0:T(8,128)(2,1)}, f32[256,5632]{1,0:T(8,128)}, f32[704,2048]{1,0:T(8,128)}, bf16[8,256,5632]{2,1,0:T(8,128)(2,1)}, bf16[5632,20...) custom-call(bf16[256,5632]{1,0:T(8,128)(2,1)} %bitcast.12, ...), custom_call_target="tpu_custom_call" | custom-call | tf_op jit(solution)/shard_map/mlp_step/pallas_call | solution.py:482
  580.6 0.0 copy-start.1
  580.6 6.8 %copy.10 = bf16[3,512,2048]{2,1,0:T(8,128)(2,1)} copy(bf16[3,512,2048]{2,1,0:T(8,128)(2,1)} %bitcast.9) | data formatting | bytes 12582912
  587.3 0.0 copy-done.1
  587.3 0.0 copy-start
  587.3 2.9 copy.11
  590.3 1.8 copy-done
  592.0 2.5 copy.12
Async XLA Ops:
  580.6 6.8 %copy-start.1 = (f32[256,5632]{1,0:T(8,128)S(1)}, f32[256,5632]{1,0:T(8,128)}, u32[]{:S(2)}) copy-start(f32[256,5632]{1,0:T(8,128)} %get-tuple-element.7) | copy-start | bytes 17301508
  587.3 4.7 copy-start

commit v2 on v1

--- a/solution.py
+++ b/solution.py
@@ -11,12 +11,13 @@
 F32 = jnp.float32
 BF16 = jnp.bfloat16
 N_CHUNK = 11
+LAG_H = 2
 LAG_T = 4
 LAG_Z = 8
 N_K = 8
 N_H = 3
 N_T = 4
-Y_STEP = 5
+Y_STEP = 6
 GELU_C = math.sqrt(2.0 / math.pi)
 NN = (((1,), (0,)), ((), ()))
 NT_DIMS = (((1,), (1,)), ((), ()))
@@ -60,7 +61,7 @@
 
     sib, xn, yn = dev(0, 0, 1), dev(0, 1, 0), dev(1, 0, 0)
     diag = dev(1, 1, 0)
-    origins = (xn, yn, diag, sib, dev(0, 1, 1), dev(1, 0, 1), dev(1, 1, 1))
+    origins = (xn, yn, diag, sib, dev(0, 1, 1), dev(1, 0, 1), dev(1, 1, 1), diag)
 
     def remote(src, dst, ssem, rsem, to):
         return pltpu.make_async_remote_copy(src_ref=src, dst_ref=dst, send_sem=ssem, recv_sem=rsem,
@@ -74,9 +75,12 @@
     def w1_cols(p):
         return pl.ds(pieces[p][0] * fc, pieces[p][1] * fc)
 
+    half = d_blk // 2
+
     def w1_copy(kind, p, origin, to, own=False):
-        src = w1.at[:, w1_cols(p)] if own else w1f.at[origin, :, w1_cols(p)]
-        return remote(src, w1f.at[origin, :, w1_cols(p)], w1_ss.at[kind, p], w1_rs.at[kind, p], to)
+        rows = pl.ds(0, half) if kind == 2 else pl.ds(half, half) if kind == 7 else pl.ds(0, d_blk)
+        src = w1.at[rows, w1_cols(p)] if own else w1f.at[origin, rows, w1_cols(p)]
+        return remote(src, w1f.at[origin, rows, w1_cols(p)], w1_ss.at[kind, p], w1_rs.at[kind, p], to)
 
     def w2_copy(kind, p, origin, to, own=False):
         rows = aligned(p * p_rows, p_rows)
@@ -89,6 +93,16 @@
 
     def w2_recv(kind, p):
         w2_copy(kind, p, origins[kind], me).wait_recv()
+
+    def w2_forward(p):
+        w2_recv(0, p)
+        if p % 2:
+            w2_copy(2, p, xn, yn).start()
+        w2_copy(4, p, xn, sib).start()
+        w2_recv(1, p)
+        if not p % 2:
+            w2_copy(2, p, yn, xn).start()
+        w2_copy(5, p, yn, sib).start()
 
     def own_w1(p):
         w1_copy(0, p, me, xn, own=True).start()
@@ -184,17 +198,16 @@
 
         def diag_forward(p):
             w1_recv(2, p)
+            w1_recv(7, p)
             w1_copy(6, p, diag, sib).start()
 
         for p in range(n_piece):
             w1_recv(0, p)
+            w1_copy(7, p, xn, yn).start()
             w1_copy(4, p, xn, sib).start()
-            if p % 2:
-                w1_copy(2, p, xn, yn).start()
             w1_recv(1, p)
+            w1_copy(2, p, yn, xn).start()
             w1_copy(5, p, yn, sib).start()
-            if not p % 2:
-                w1_copy(2, p, yn, xn).start()
             if p + 2 < n_piece:
                 own_w1(p + 2)
             else:
@@ -205,9 +218,12 @@
                 compute(p - 2)
         own_w2(2)
         own_w2(3)
+        w2_forward(0)
         diag_forward(n_piece - 1)
         compute(n_piece - 2)
+        w2_forward(1)
         compute(n_piece - 1)
+        w2_forward(2)
         for k in (N_CHUNK - 2, N_CHUNK - 1):
             for cp in stores(k, k % 2):
                 cp.wait()
@@ -237,6 +253,9 @@
 
         def send_t(q):
             return remote(t_b.at[q % N_T], r_t.at[q], t_ss.at[q % N_T], c_rs.at[2, q], second_dev(q))
+
+        def sib_load(q):
+            return pltpu.make_async_copy(r_s.at[q], st_s, io_sem.at[0])
 
         def lhs_loads(q):
             cps = []
@@ -272,18 +291,15 @@
             cp.start()
 
         def step(s, _):
-            @pl.when(s < n_piece)
-            def _():
-                w2_recv(0, s)
-                w2_copy(4, s, xn, sib).start()
-                w2_recv(1, s)
-                w2_copy(5, s, yn, sib).start()
-                w2_copy(2, s, pick(s % 2, yn, xn), pick(s % 2, xn, yn)).start()
-
-            @pl.when((s >= 1) & (s < n_piece + 1))
-            def _():
-                w2_recv(2, s - 1)
-                w2_copy(6, s - 1, diag, sib).start()
+            @pl.when(s == 1)
+            def _():
+                w2_forward(3)
+
+            @pl.when(s == Y_STEP - 1)
+            def _():
+                for p in range(n_piece):
+                    w2_recv(2, p)
+                    w2_copy(6, p, diag, sib).start()
 
             @pl.when(s == Y_STEP)
             def _():
@@ -295,21 +311,18 @@
                 for cp in e_loads(0):
                     cp.start()
 
-            @pl.when((s >= 1) & (s - 1 < n_q))
-            def _():
-                q = s - 1
-                send_s(q).wait_recv()
-                ld = pltpu.make_async_copy(r_s.at[q], st_s, io_sem.at[0])
-                ld.start()
+            @pl.when((s >= LAG_H) & (s - LAG_H < n_q))
+            def _():
+                q = s - LAG_H
 
                 @pl.when(q >= N_H)
                 def _():
                     send_h(q - N_H).wait_send()
 
-                ld.wait()
-                h_b[q % N_H] = m_b[0:2] + st_s[0:2]
-                k_b[q % N_K] = m_b[2:4] + st_s[2:4]
+                sib_load(q).wait()
+                h_b[q % N_H] = m_b[q % 2, 0:2] + st_s[0:2]
                 send_h(q).start()
+                k_b[q % N_K] = m_b[q % 2, 2:4] + st_s[2:4]
 
             @pl.when((s >= LAG_T) & (s - LAG_T < n_q))
             def _():
@@ -365,7 +378,7 @@
                     rows = aligned(n * r2, r2)
                     for b in range(4):
                         s_b[s % 2, b, rows, :] = res[b * r2:(b + 1) * r2]
-                        m_b[b, rows, :] = res[(4 + b) * r2:(5 + b) * r2]
+                        m_b[s % 2, b, rows, :] = res[(4 + b) * r2:(5 + b) * r2]
                     return 0
 
                 lax.fori_loop(0, n_tile, tile, 0)
@@ -400,7 +413,7 @@
                         cp.start()
 
                 for b, mb in enumerate(chips_of(s)):
-                    for cc, dst in ((1 - core, s_b.at[s % 2]), (core, m_b)):
+                    for cc, dst in ((1 - core, s_b.at[s % 2]), (core, m_b.at[s % 2])):
                         rows = aligned(d_blk * (2 * mb + cc), d_blk)
                         dst[b] = matmul(x_v[:, rows], q_v[...], TN_DIMS)
                 send_s(s).start()
@@ -430,6 +443,11 @@
                     cp = pltpu.make_async_copy(hy, y.at[:, n * fc:(n + 1) * fc], ld_sem.at[4])
                     cp.start()
                     cp.wait()
+
+            @pl.when((s + 1 >= LAG_H) & (s + 1 - LAG_H < n_q))
+            def _():
+                send_s(s + 1 - LAG_H).wait_recv()
+                sib_load(s + 1 - LAG_H).start()
 
             return 0
 
@@ -444,16 +462,17 @@
         z_wait(n_q - 1)
 
     blk = (d_blk, fc)
-    pl.run_scoped(main, pltpu.VMEM((2, 4) + blk, F32), pltpu.VMEM((4,) + blk, F32), pltpu.VMEM((N_K, 2) + blk, F32),
+    pl.run_scoped(main, pltpu.VMEM((2, 4) + blk, F32), pltpu.VMEM((2, 4) + blk, F32), pltpu.VMEM((N_K, 2) + blk, F32),
                   pltpu.VMEM((N_H, 2) + blk, F32), pltpu.VMEM((N_T,) + blk, F32), pltpu.VMEM((2,) + blk, F32),
                   pltpu.VMEM((4,) + blk, F32), pltpu.VMEM((2,) + blk, F32), pltpu.VMEM(blk, F32),
                   pltpu.VMEM((tokens, fc), BF16), pltpu.VMEM((8, r2, tokens), BF16),
                   pltpu.VMEM((fc, d_model), BF16), pltpu.VMEM((tokens, fc), BF16),
                   pltpu.VMEM((fc, d_model), BF16), pltpu.VMEM((tokens, fc), BF16))
 
-    for kind in range(7):
-        for p in range(n_piece):
+    for p in range(n_piece):
+        for kind in range(8):
             w1_copy(kind, p, me, sib).wait_send()
+        for kind in range(7):
             w2_copy(kind, p, me, sib).wait_send()
 
 
@@ -488,7 +507,7 @@
             pltpu.VMEM((tokens, d_model), BF16),
             pltpu.VMEM((tokens, d_model), BF16),
             pltpu.VMEM((tokens, d_model), F32),
-            dma((7, 4)), dma((7, 4)), dma((7, 4)), dma((7, 4)),
+            dma((8, 4)), dma((8, 4)), dma((7, 4)), dma((7, 4)),
             dma((3, n_q)), dma((2,)), dma((N_H,)), dma((N_T,)),
             dma((3, 2)), dma((2,)), dma((4,)), dma((5,)),
         ],

time: 597 us -> 586 us (0.982)
  Pallas kernels: 580 us -> 569 us
    pallas_call x1, Pallas kernels: 580 us -> 569 us  [fused_step(): pl.pallas_call(functools.partial(kernel, (tokens, d_model, d_ff)), out_sh...]
where the time goes in v2:
time: 586 us; the launch traced here: 584 us
  Pallas kernels  569 us (97%)
  local copies, waits for them, and re-layouts  14 us (2%)
    pallas_call x1, Pallas kernels, fused_step(): pl.pallas_call(functools.partial(kernel, (tokens, d_model, d_ff)), out_sh...  569 us
    unnamed x7, local copies, waits for them, and re-layouts  14 us

profile of v2, /device:TPU:0, one launch (start us, length us, event | category | flops | bytes accessed | tf_op | source)
XLA Modules:
  0.0 583.9 jit_solution(4658095618913014611)
XLA Ops:
  0.6 569.2 %mlp_step.1 = (bf16[1536,2048]{1,0:T(8,128)(2,1)}, f32[256,5632]{1,0:T(8,128)}, f32[704,2048]{1,0:T(8,128)}, bf16[8,256,5632]{2,1,0:T(8,128)(2,1)}, bf16[5632,20...) custom-call(bf16[256,5632]{1,0:T(8,128)(2,1)} %bitcast.12, ...), custom_call_target="tpu_custom_call" | custom-call | tf_op jit(solution)/shard_map/mlp_step/pallas_call | solution.py:501
  569.9 0.0 copy-start.1
  569.9 6.8 %copy.10 = bf16[3,512,2048]{2,1,0:T(8,128)(2,1)} copy(bf16[3,512,2048]{2,1,0:T(8,128)(2,1)} %bitcast.9) | data formatting | bytes 12582912
  576.7 0.0 copy-done.1
  576.7 0.0 copy-start
  576.7 2.9 copy.11
  579.6 1.8 copy-done
  581.4 2.5 copy.12
Async XLA Ops:
  569.9 6.8 %copy-start.1 = (f32[256,5632]{1,0:T(8,128)S(1)}, f32[256,5632]{1,0:T(8,128)}, u32[]{:S(2)}) copy-start(f32[256,5632]{1,0:T(8,128)} %get-tuple-element.7) | copy-start | bytes 17301508
  576.7 4.7 copy-start

commit v3 on v0

v3 whole, which is shorter than its diff:
```python
import functools
import math

import jax
import jax.numpy as jnp
from jax import lax
from jax.experimental import pallas as pl
from jax.experimental.pallas import tpu as pltpu
from jax.sharding import PartitionSpec as P

F32 = jnp.float32
BF16 = jnp.bfloat16
N_CHUNK = 11
N_FOUR = 6
N_DOWN = N_CHUNK - N_FOUR
N_PAIR = N_DOWN + N_CHUNK
N_PRE = 5
LAG_Z = 6
N_K = 5
N_H = 6
N_SPLIT = 8
T_STEP = 11
GELU_C = math.sqrt(2.0 / math.pi)
NN = (((1,), (0,)), ((), ()))
NT = (((1,), (1,)), ((), ()))
TN = (((0,), (0,)), ((), ()))


def matmul(a, b, dims=NN):
    return lax.dot_general(a, b, dims, preferred_element_type=F32)


def aligned(start, size):
    return pl.ds(pl.multiple_of(start, size), size)


def gelu_parts(u):
    p = GELU_C + (GELU_C * 0.044715) * (u * u)
    t = jnp.tanh(u * p)
    return t, p


def gelu_hidden(u):
    t, _ = gelu_parts(u)
    return u * (0.5 * (1.0 + t))


def gelu_slope(u):
    t, p = gelu_parts(u)
    return 0.5 * (1.0 + t), (0.5 * u * (1.0 - t * t)) * (3.0 * p - 2.0 * GELU_C)


def kernel(sizes, w1, w2, x, g, y, gup, gdown,
           w1f, w2f, x_l, g_l, a_h, ht_h, a2_h, ht2_h, q_h, q2_h, r_s4, r_h4, r_t4, h_h4, k_h4, t_h4, r_sp, r_hp,
           x_v, g_v, x_n, g_n, y_acc,
           w1_ss, w1_rs, w2_ss, w2_rs, tk_ss, tk_rs, four_ss, four_rs, s_ss, hp_ss, sp_rs, hp_rs, io, ld, out_sem):
    tokens, d_model, d_ff = sizes
    fc = d_ff // N_CHUNK
    hc = fc // 2
    d_blk = d_model // 8
    f_blk = d_ff // 8
    r2 = f_blk // N_CHUNK
    n_tile = d_model // fc
    row_t = tokens // 3
    n_row = 3
    pieces = ((0, 2), (2, 3), (5, 3), (8, 3))
    n_piece = 4
    p_rows = f_blk // n_piece

    me = lax.axis_index('fsdp')
    core = me % 2
    cx = (me // 2) % 2
    cy = me // 4
    chip = me // 2

    def at(yy, xx, cc):
        return 4 * yy + 2 * xx + cc

    oy, ox, oc = 1 - cy, 1 - cx, 1 - core
    sib, xn, yn, diag = at(cy, cx, oc), at(cy, ox, core), at(oy, cx, core), at(oy, ox, core)
    chip_x = xn // 2
    w1_org = (xn, yn, diag, sib, at(cy, ox, oc), at(oy, cx, oc), at(oy, ox, oc))
    w2_org = (xn, at(oy, 0, core), at(oy, 1, core), sib, at(cy, ox, oc), at(oy, 0, oc), at(oy, 1, oc))

    def remote(src, dst, ssem, rsem, to):
        return pltpu.make_async_remote_copy(src_ref=src, dst_ref=dst, send_sem=ssem, recv_sem=rsem,
                                            device_id=(to,), device_id_type=pl.DeviceIdType.MESH)

    def local(src, dst, sem):
        return pltpu.make_async_copy(src, dst, sem)

    barrier = pltpu.get_barrier_semaphore()
    for other in (sib, xn, yn):
        pl.semaphore_signal(barrier, inc=1, device_id=(other,), device_id_type=pl.DeviceIdType.MESH)
    pl.semaphore_wait(barrier, 3)

    def w1_cols(p):
        return pl.ds(pieces[p][0] * fc, pieces[p][1] * fc)

    def w1_copy(kind, p, origin, to, own=False):
        src = w1.at[:, w1_cols(p)] if own else w1f.at[origin, :, w1_cols(p)]
        return remote(src, w1f.at[origin, :, w1_cols(p)], w1_ss.at[kind, p], w1_rs.at[kind, p], to)

    def w2_copy(kind, p, origin, to, own=False):
        rows = aligned(p * p_rows, p_rows)
        full = aligned(origin * f_blk + p * p_rows, p_rows)
        src = w2.at[rows, :] if own else w2f.at[full, :]
        return remote(src, w2f.at[full, :], w2_ss.at[kind, p], w2_rs.at[kind, p], to)

    def token_copy(n):
        src, dst = (x, x_l) if n < 3 else (g, g_l)
        rows = pl.ds((n % 3) * row_t, row_t)
        return remote(src.at[rows, :], dst.at[rows, :], tk_ss.at[n], tk_rs.at[n], yn)

    def w1_recv(kind, p):
        w1_copy(kind, p, w1_org[kind], me).wait_recv()

    def w2_recv(kind, p):
        w2_copy(kind, p, w2_org[kind], me).wait_recv()

    for p in range(n_piece):
        w1_copy(0, p, me, xn, own=True).start()
        w1_copy(1, p, me, yn, own=True).start()
    for n in range(6):
        token_copy(n).start()
    for p in range(n_piece):
        w1_copy(3, p, me, sib, own=True).start()
    for p in range(n_piece):
        w2_copy(3, p, me, sib, own=True).start()

    load_x = local(x, x_v, io.at[0])
    load_g = local(g, g_v, io.at[1])
    load_x.start()
    load_g.start()

    def stage_own(buf1, buf2):
        in1 = local(w1, buf1, io.at[2])
        in2 = local(w2, buf2, io.at[3])
        in1.start()
        in2.start()
        in1.wait()
        out1 = local(buf1, w1f.at[me], io.at[2])
        out1.start()
        in2.wait()
        out2 = local(buf2, w2f.at[aligned(me * f_blk, f_blk), :], io.at[3])
        out2.start()
        out1.wait()
        out2.wait()

    pl.run_scoped(stage_own, pltpu.VMEM((d_blk, d_ff), BF16), pltpu.VMEM((f_blk, d_model), BF16))
    load_x.wait()
    load_g.wait()

    def init_rows(r, c):
        rows = aligned(r * row_t, row_t)
        y_acc[rows, :] = x_v[rows, :].astype(F32)
        return c

    lax.fori_loop(0, n_row, init_rows, ())

    def pass_one(x_ref, a_dst, ht_dst, wb, ab, htb):
        def w1_load(k, slot):
            return local(w1f.at[:, :, aligned(k * fc, fc)], wb.at[slot], ld.at[slot])

        def stores(k, slot):
            cols = aligned(k * fc, fc)
            return (local(ab.at[slot], a_dst.at[:, cols], out_sem.at[slot]),
                    local(htb.at[slot], ht_dst.at[cols, :], out_sem.at[2 + slot]))

        def run(ready):
            def chunk(k, c):
                slot = k % 2
                for p, (first, count) in enumerate(pieces):
                    @pl.when(k == first)
                    def _():
                        ready(p)
                        w1_load(k, slot).start()

                w1_load(k, slot).wait()
                for first, count in pieces:
                    @pl.when((k >= first) & (k + 1 < first + count))
                    def _():
                        w1_load(k + 1, 1 - slot).start()

                @pl.when(k >= 2)
                def _():
                    for cp in stores(k - 2, slot):
                        cp.wait()

                def rows_loop(r, c):
                    rows = aligned(r * row_t, row_t)
                    acc = matmul(x_ref[rows, :], wb[slot].reshape(d_model, fc)).astype(BF16)
                    ab[slot, rows, :] = acc
                    u = acc.astype(F32)
                    htb[slot, :, rows] = gelu_hidden(u).astype(BF16).T
                    return c

                lax.fori_loop(0, n_row, rows_loop, (), unroll=True)
                for cp in stores(k, slot):
                    cp.start()
                return c

            lax.fori_loop(0, N_CHUNK, chunk, ())

        def finish():
            for k in (N_CHUNK - 2, N_CHUNK - 1):
                for cp in stores(k, k % 2):
                    cp.wait()

        return run, finish

    pass_bufs = (pltpu.VMEM((2, 8, d_blk, fc), BF16), pltpu.VMEM((2, tokens, fc), BF16), pltpu.VMEM((2, fc, tokens), BF16))

    def own_pass(wb, ab, htb):
        run, finish = pass_one(x_v, a_h, ht_h, wb, ab, htb)
        for p in range(n_piece):
            w1_recv(0, p)
            w1_copy(4, p, xn, sib).start()
            w1_recv(1, p)
            w1_copy(2, p, yn, xn).start()
            w1_copy(5, p, yn, sib).start()
        for p in range(n_piece):
            w2_copy(0, p, me, xn, own=True).start()
        def ready(p):
            w1_recv(2, p)
            w1_copy(6, p, diag, sib).start()
            for kind in (3, 4, 5, 6):
                w1_recv(kind, p)

        run(ready)
        finish()

    pl.run_scoped(own_pass, *pass_bufs)

    blk = (d_blk, fc)

    def s4_copy(src, q):
        return remote(src, r_s4.at[q], s_ss.at[q % 2], four_rs.at[0, q], sib)

    def h4_copy(q):
        return remote(h_h4.at[q], r_h4.at[q], four_ss.at[0, q], four_rs.at[1, q], xn)

    def t4_copy(q):
        return remote(t_h4.at[q], r_t4.at[q], four_ss.at[1, q], four_rs.at[2, q], yn)

    def lhs_loads(k, chips, src, dst, sem):
        cps = []
        n = len(chips)
        for cc in range(2):
            for b, mb in enumerate(chips):
                rows = aligned(f_blk * (2 * mb + cc) + r2 * k, r2)
                cps.append(local(src.at[rows, :], dst.at[n * cc + b], sem))
        return cps

    def four(sm, st_s, hk, lhs):
        chips = (chip_x, diag // 2, chip, yn // 2)

        def send_s(q):
            return s4_copy(sm.at[q % 2, oc], q)

        def sib_load(q):
            return local(r_s4.at[q], st_s, io.at[0])

        def stores(q):
            return (local(hk.at[q % 2, pl.ds(0, 2)], h_h4.at[q], out_sem.at[q % 2]),
                    local(hk.at[q % 2, pl.ds(2, 2)], k_h4.at[q], out_sem.at[2 + q % 2]))

        for cp in lhs_loads(0, chips, ht_h, lhs, ld.at[0]):
            cp.start()

        def step(s, c):
            @pl.when((s >= 3) & (s - 3 < N_FOUR))
            def _():
                for cp in stores(s - 3):
                    cp.wait()
                h4_copy(s - 3).start()

            @pl.when((s >= 2) & (s - 2 < N_FOUR))
            def _():
                q = s - 2
                sib_load(q).wait()
                hk[q % 2] = sm[q % 2, core] + st_s[...]
                for cp in stores(q):
                    cp.start()
                send_s(q).wait_send()

            @pl.when(s < N_FOUR)
            def _():
                local(lhs, lhs, ld.at[0]).wait()

                def tile(n, c):
                    res = matmul(lhs[...].reshape(8 * r2, tokens), g_v[:, aligned(n * fc, fc)])
                    rows = aligned(n * r2, r2)
                    for b in range(8):
                        sm[s % 2, b // 4, b % 4, rows, :] = res[b * r2:(b + 1) * r2]
                    return c

                lax.fori_loop(0, n_tile, tile, ())
                send_s(s).start()

                @pl.when(s + 1 < N_FOUR)
                def _():
                    for cp in lhs_loads(s + 1, chips, ht_h, lhs, ld.at[0]):
                        cp.start()

            @pl.when((s >= 1) & (s - 1 < N_FOUR))
            def _():
                send_s(s - 1).wait_recv()
                sib_load(s - 1).start()

            return c

        lax.fori_loop(0, N_FOUR + 3, step, ())

    pl.run_scoped(four, pltpu.VMEM((2, 2, 4) + blk, F32), pltpu.VMEM((4,) + blk, F32),
                  pltpu.VMEM((2, 4) + blk, F32), pltpu.VMEM((8, r2, tokens), BF16))

    for p in range(n_piece):
        w2_recv(0, p)
        w2_copy(4, p, xn, sib).start()
    for kind in (1, 2):
        for p in range(n_piece):
            w2_copy(kind, p, at(cy, kind - 1, core), yn).start()

    def half_cols(j, h):
        return aligned((cy * (d_ff // 2) + fc * j + hc * h) % d_ff, hc)

    def y_job(w2c, a_ref):
        def rows_loop(r, c):
            rows = aligned(r * row_t, row_t)
            u = a_ref[rows, :].astype(F32)
            y_acc[rows, :] += matmul(gelu_hidden(u).astype(BF16), w2c[...])
            return c

        lax.fori_loop(0, n_row, rows_loop, (), unroll=True)

    def own_job(w2c, a_ref, q_dst, with_y=True, unroll=False):
        def rows_loop(r, c):
            rows = aligned(r * row_t, row_t)
            e = matmul(g_v[rows, :], w2c[...], NT)
            u = a_ref[rows, :].astype(F32)
            cdf, rest = gelu_slope(u)
            q_dst[rows, :] = (e * (cdf + rest)).astype(BF16)
            if with_y:
                y_acc[rows, :] += matmul((u * cdf).astype(BF16), w2c[...])
            return c

        lax.fori_loop(0, n_row, rows_loop, (), unroll=unroll)

    def nbr_job(w2c, a_ref, q_dst, first, last, unroll=False):
        def rows_loop(r, c):
            rows = aligned(r * row_t, row_t)
            e = matmul(g_n[rows, :], w2c[...], NT)
            cdf, rest = gelu_slope(a_ref[rows, :].astype(F32))
            q_dst[rows, :] = (e * (cdf + rest)).astype(BF16)
            return c

        lax.fori_loop(first, last, rows_loop, (), unroll=unroll)

    def w2_loads(j, dst, sem):
        return [local(w2f.at[half_cols(j, h), :], dst.at[pl.ds(h * hc, hc), :], sem) for h in range(2)]

    def a_loads(j, src, dst, sem):
        return [local(src.at[:, half_cols(j, h)], dst.at[:, pl.ds(h * hc, hc)], sem) for h in range(2)]

    def start_all(cps):
        for cp in cps:
            cp.start()

    def pre_jobs(w2c, a_c, q_c):
        for p in range(n_piece):
            for kind in (3, 4):
                w2_recv(kind, p)
        start_all(w2_loads(0, w2c.at[0], ld.at[0]) + a_loads(0, a_h, a_c.at[0], ld.at[2]))

        def job(j, c):
            slot = j % 2
            local(w2c.at[slot], w2c.at[slot], ld.at[slot]).wait()
            local(a_c.at[slot], a_c.at[slot], ld.at[2 + slot]).wait()

            @pl.when(j + 1 < N_PRE)
            def _():
                start_all(w2_loads(j + 1, w2c.at[1 - slot], ld.at[1 - slot]) +
                          a_loads(j + 1, a_h, a_c.at[1 - slot], ld.at[3 - slot]))

            @pl.when(j >= 2)
            def _():
                local(q_c.at[slot], q_h.at[j - 2], out_sem.at[slot]).wait()

            own_job(w2c.at[slot], a_c.at[slot], q_c.at[slot])
            local(q_c.at[slot], q_h.at[j], out_sem.at[slot]).start()
            return c

        lax.fori_loop(0, N_PRE, job, ())
        for j in (N_PRE - 2, N_PRE - 1):
            local(q_c.at[j % 2], q_h.at[j], out_sem.at[j % 2]).wait()

    pl.run_scoped(pre_jobs, pltpu.VMEM((2, fc, d_model), BF16), pltpu.VMEM((2, tokens, fc), BF16),
                  pltpu.VMEM((2, tokens, fc), BF16))

    for n in range(3):
        token_copy(n).wait_recv()
    cp = local(x_l, x_n, io.at[0])
    cp.start()
    cp.wait()

    def nbr_pass(wb, ab, htb):
        run, finish = pass_one(x_n, a2_h, ht2_h, wb, ab, htb)
        run(lambda p: None)
        finish()

    pl.run_scoped(nbr_pass, *pass_bufs)

    part = tokens - row_t

    def pre_nbr(w2c, a_c, q_c):
        for n in range(3, 5):
            token_copy(n).wait_recv()
        load = local(g_l.at[pl.ds(0, part), :], g_n.at[pl.ds(0, part), :], io.at[2])
        load.start()
        start_all(w2_loads(0, w2c.at[0], ld.at[0]) + a_loads(0, a2_h, a_c.at[0], ld.at[2]))
        load.wait()

        def store(j):
            return local(q_c.at[j % 2, pl.ds(0, part), :], q2_h.at[j], out_sem.at[j % 2])

        def job(j, c):
            slot = j % 2
            local(w2c.at[slot], w2c.at[slot], ld.at[slot]).wait()
            local(a_c.at[slot], a_c.at[slot], ld.at[2 + slot]).wait()

            @pl.when(j + 1 < N_PRE)
            def _():
                start_all(w2_loads(j + 1, w2c.at[1 - slot], ld.at[1 - slot]) +
                          a_loads(j + 1, a2_h, a_c.at[1 - slot], ld.at[3 - slot]))

            @pl.when(j >= 2)
            def _():
                store(j - 2).wait()

            nbr_job(w2c.at[slot], a_c.at[slot], q_c.at[slot], 0, n_row - 1)
            store(j).start()
            return c

        lax.fori_loop(0, N_PRE, job, ())
        for j in (N_PRE - 2, N_PRE - 1):
            store(j).wait()

    pl.run_scoped(pre_nbr, pltpu.VMEM((2, fc, d_model), BF16), pltpu.VMEM((2, tokens, fc), BF16),
                  pltpu.VMEM((2, tokens, fc), BF16))

    def second_sum(q, st_k, st_r):
        h4_copy(q).wait_recv()
        c1 = local(k_h4.at[q], st_k, io.at[2])
        c2 = local(r_h4.at[q], st_r, io.at[3])
        c1.start()
        c2.start()
        c1.wait()
        c2.wait()
        st_r[...] = st_k[...] + st_r[...]
        c1 = local(st_r.at[1], t_h4.at[q], io.at[2])
        c2 = local(st_r.at[0], k_h4.at[q, 0], io.at[3])
        c1.start()
        c2.start()
        c1.wait()
        c2.wait()

    n_early = N_FOUR - 1

    def four_second(st_k, st_r):
        def item(q, c):
            second_sum(q, st_k, st_r)
            return c

        lax.fori_loop(0, n_early, item, ())

    pl.run_scoped(four_second, pltpu.VMEM((2,) + blk, F32), pltpu.VMEM((2,) + blk, F32))

    def pair(sm, h_b, k_b, st_s, st_h, z_b, qa, q_n, lhs, w2c, a_n, qt):
        chips = (chip_x, chip)

        def send_s(i):
            return remote(sm.at[i % 2, oc], r_sp.at[i], s_ss.at[i % 2], sp_rs.at[i], sib)

        def send_h(i):
            return remote(h_b.at[i % N_H], r_hp.at[i], hp_ss.at[i % N_H], hp_rs.at[i], xn)

        def sib_load(i):
            return local(r_sp.at[i], st_s, io.at[0])

        def hop_load(i):
            return local(r_hp.at[i], st_h, io.at[1])

        def mid(s):
            @pl.when((s >= 1) & (s <= N_PAIR))
            def _():
                send_s(s - 1).wait_recv()
                sib_load(s - 1).start()

            @pl.when((s + 1 >= LAG_Z) & (s + 1 - LAG_Z < N_PAIR))
            def _():
                send_h(s + 1 - LAG_Z).wait_recv()
                hop_load(s + 1 - LAG_Z).start()

        def hop(s):
            @pl.when((s >= 1) & (s <= N_PAIR))
            def _():
                i = s - 1

                @pl.when(i >= N_H)
                def _():
                    send_h(i - N_H).wait_send()

                sib_load(i).wait()
                h_b[i % N_H] = sm[i % 2, core, 0] + st_s[0]
                send_h(i).start()
                k_b[i % N_K] = sm[i % 2, core, 1] + st_s[1]

        def last_loads(q):
            slot = q % 2
            return (local(k_h4.at[q, 0], qt.at[slot, 0], io.at[2 + slot]), local(r_t4.at[q], qt.at[slot, 1], io.at[2 + slot]))

        def last_start(q):
            t4_copy(q).wait_recv()
            start_all(last_loads(q))

        def last(q):
            slot = q % 2
            local(qt.at[slot], qt.at[slot], io.at[2 + slot]).wait()
            z_wait(slot)
            z_b[slot] = qt[slot, 0] + qt[slot, 1]
            z_down(q, slot)

        def pair_lhs(i):
            return (lhs_loads(N_FOUR + i, chips, ht_h, lhs.at[0], ld.at[0]) +
                    lhs_loads(N_FOUR + i, chips, ht2_h, lhs.at[1], ld.at[0]))

        def z_wait(slot):
            local(z_b.at[slot], gup.at[:, pl.ds(0, fc)], out_sem.at[slot]).wait()

        def z_down(k, slot):
            start_all([local(z_b.at[slot, n * r2:(n + 1) * r2, :],
                             gdown.at[aligned(k * r2, r2), n * fc:(n + 1) * fc], out_sem.at[slot])
                       for n in range(n_tile)])

        def z_up(j, slot):
            start_all([local(z_b.at[slot, :, h * hc:(h + 1) * hc], gup.at[:, half_cols(j, h)], out_sem.at[slot])
                       for h in range(2)])

        def up_loads(j):
            return w2_loads(j, w2c, ld.at[1]) + a_loads(j, a2_h, a_n, ld.at[2])

        def q2_load(j):
            return local(q2_h.at[j], q_n.at[pl.ds(0, part), :], ld.at[0])

        start_all(pair_lhs(0) + up_loads(0))
        local(q_h.at[0], qa.at[1], ld.at[3]).start()
        token_copy(5).wait_recv()
        load_n = local(g_l.at[pl.ds(part, row_t), :], g_n.at[pl.ds(part, row_t), :], io.at[2])
        load_n.start()
        load_n.wait()

        def step(s, c):
            @pl.when(s >= LAG_Z)
            def _():
                i = s - LAG_Z
                @pl.when(i >= 2)
                def _():
                    z_wait(i % 2)

                hop_load(i).wait()
                z_b[i % 2] = k_b[i % N_K] + st_h[...]

                @pl.when(i < N_DOWN)
                def _():
                    z_down(N_FOUR + i, i % 2)

                @pl.when(i >= N_DOWN)
                def _():
                    z_up(i - N_DOWN, i % 2)

            @pl.when((s >= 2) & (s < N_PAIR))
            def _():
                send_s(s - 2).wait_send()

            @pl.when(s < N_DOWN)
            def _():
                local(lhs, lhs, ld.at[0]).wait()

                @pl.when(s == 1)
                def _():
                    mid(s)
                    hop(s)

                def tile(n, c):
                    cols = aligned(n * fc, fc)
                    rows = aligned(n * r2, r2)
                    res = (matmul(lhs[0].reshape(4 * r2, tokens), g_v[:, cols]) +
                           matmul(lhs[1].reshape(4 * r2, tokens), g_n[:, cols]))
                    for b in range(4):
                        sm[s % 2, b // 2, b % 2, rows, :] = res[b * r2:(b + 1) * r2]

                    @pl.when((n == 1) & (s > 1))
                    def _():
                        mid(s)

                    @pl.when((n == 2) & (s > 1))
                    def _():
                        hop(s)

                    return c

                lax.fori_loop(0, n_tile, tile, ())
                send_s(s).start()

                @pl.when(s + 1 < N_DOWN)
                def _():
                    start_all(pair_lhs(s + 1))

                @pl.when(s + 1 == N_DOWN)
                def _():
                    q2_load(0).start()

            @pl.when(s == N_DOWN + N_PRE - 2)
            def _():
                second_sum(N_FOUR - 1, qt.at[0], qt.at[1])

            @pl.when((s >= T_STEP) & (s < T_STEP + N_FOUR))
            def _():
                t4_copy(s - T_STEP).start()

            @pl.when((s >= N_DOWN) & (s < N_PAIR))
            def _():
                j = s - N_DOWN
                pre = (N_PRE + N_CHUNK - 1 - j) // N_CHUNK
                q_slot = pre * ((j + 1) % 2) + (1 - pre)
                local(w2c, w2c, ld.at[1]).wait()
                local(a_n, a_n, ld.at[2]).wait()
                local(qa.at[0], qa.at[0], ld.at[3]).wait()

                @pl.when(j < N_PRE)
                def _():
                    q2_load(j).wait()


                @pl.when(j < N_PRE)
                def _():
                    nbr_job(w2c, a_n, q_n, n_row - 1, n_row)

                @pl.when(j >= N_PRE)
                def _():
                    nbr_job(w2c, a_n, q_n, 0, n_row, unroll=True)

                mid(s)

                @pl.when(j == N_PRE - 2)
                def _():
                    for p in range(n_piece):
                        w2_recv(1, p)
                        w2_copy(5, p, w2_org[1], sib).start()

                @pl.when((j >= N_PRE) & (j < N_SPLIT))
                def _():
                    own_job(w2c, qa.at[0], qa.at[1])
                    hop(s)

                @pl.when(j >= N_SPLIT)
                def _():
                    own_job(w2c, qa.at[0], qa.at[1], with_y=False, unroll=True)
                    hop(s)

                @pl.when(j == N_SPLIT - 1)
                def _():
                    for p in range(n_piece):
                        w2_recv(2, p)
                        w2_copy(6, p, w2_org[2], sib).start()

                @pl.when(j + 1 == N_PRE)
                def _():
                    for p in range(n_piece):
                        w2_recv(5, p)

                @pl.when((j + 1 < N_CHUNK) & (j + 1 != N_SPLIT))
                def _():
                    start_all(up_loads(j + 1))

                @pl.when(j + 1 < N_PRE)
                def _():
                    local(q_h.at[j + 1], qa.at[j % 2], ld.at[3]).start()

                @pl.when(j + 1 == N_CHUNK)
                def _():
                    start_all(w2_loads(N_SPLIT, w2c, ld.at[1]) + a_loads(N_SPLIT, a_h, qa.at[0], ld.at[3]))

                @pl.when((j + 1 >= N_PRE) & (j + 1 < N_CHUNK))
                def _():
                    start_all(a_loads(j + 1, a_h, qa.at[0], ld.at[3]))

                for b, mb in enumerate(chips):
                    rows = aligned(2 * d_blk * mb, 2 * d_blk)
                    res = matmul(x_v[:, rows], qa[q_slot], TN) + matmul(x_n[:, rows], q_n[...], TN)
                    sm[s % 2, 0, b] = res[:d_blk]
                    sm[s % 2, 1, b] = res[d_blk:]
                send_s(s).start()

                @pl.when(j + 1 < N_PRE)
                def _():
                    q2_load(j + 1).start()

                @pl.when(j < N_PRE)
                def _():
                    hop(s)

                @pl.when(j + 1 == N_SPLIT)
                def _():
                    for p in range(n_piece):
                        w2_recv(6, p)
                    start_all(up_loads(j + 1))

            @pl.when(s >= N_PAIR)
            def _():
                mid(s)
                hop(s)

            n_late = N_CHUNK - N_SPLIT

            @pl.when((s > N_PAIR) & (s <= N_PAIR + n_late))
            def _():
                j = s - N_PAIR - 1 + N_SPLIT
                local(w2c, w2c, ld.at[1]).wait()
                local(qa.at[0], qa.at[0], ld.at[3]).wait()
                y_job(w2c, qa.at[0])

                @pl.when(j + 1 < N_CHUNK)
                def _():
                    start_all(w2_loads(j + 1, w2c, ld.at[1]) + a_loads(j + 1, a_h, qa.at[0], ld.at[3]))

            @pl.when(s == N_PAIR + n_late + 1)
            def _():
                for n in range(n_tile):
                    slot = n % 2
                    if n >= 2:
                        local(qa.at[slot], y.at[:, (n - 2) * fc:(n - 1) * fc], ld.at[2 + slot]).wait()
                    qa[slot] = y_acc[:, n * fc:(n + 1) * fc].astype(BF16)
                    local(qa.at[slot], y.at[:, n * fc:(n + 1) * fc], ld.at[2 + slot]).start()

            for half in range(2):
                @pl.when((s > N_PAIR + 1) & (s < N_PAIR + 2 + N_FOUR // 2))
                def _():
                    last(2 * (s - N_PAIR - 2) + half)

            for half in range(2):
                @pl.when((s > N_PAIR) & (s < N_PAIR + 1 + N_FOUR // 2))
                def _():
                    last_start(2 * (s - N_PAIR - 1) + half)

            return c

        lax.fori_loop(0, N_PAIR + LAG_Z, step, ())
        send_s(N_PAIR - 2).wait_send()
        send_s(N_PAIR - 1).wait_send()
        for i in range(N_PAIR - N_H, N_PAIR):
            send_h(i).wait_send()

        for n in range(n_tile - 2, n_tile):
            local(qa.at[n % 2], y.at[:, n * fc:(n + 1) * fc], ld.at[2 + n % 2]).wait()
        z_wait(0)
        z_wait(1)

    pl.run_scoped(pair, pltpu.VMEM((2, 2, 2) + blk, F32), pltpu.VMEM((N_H,) + blk, F32),
                  pltpu.VMEM((N_K,) + blk, F32), pltpu.VMEM((2,) + blk, F32), pltpu.VMEM(blk, F32),
                  pltpu.VMEM((2,) + blk, F32), pltpu.VMEM((2, tokens, fc), BF16), pltpu.VMEM((tokens, fc), BF16),
                  pltpu.VMEM((2, 4, r2, tokens), BF16), pltpu.VMEM((fc, d_model), BF16),
                  pltpu.VMEM((tokens, fc), BF16), pltpu.VMEM((2, 2) + blk, F32))

    for kind in range(7):
        for p in range(n_piece):
            w1_copy(kind, p, me, sib).wait_send()
            w2_copy(kind, p, me, sib).wait_send()
    for n in range(6):
        token_copy(n).wait_send()
    for q in range(N_FOUR):
        h4_copy(q).wait_send()
        t4_copy(q).wait_send()


def fused_step(w1, w2, x, g):
    tokens, d_model = x.shape
    d_ff = w1.shape[1]
    fc = d_ff // N_CHUNK
    d_blk = d_model // 8
    blk = (d_blk, fc)
    shape = jax.ShapeDtypeStruct
    any_spec = pl.BlockSpec(memory_space=pl.ANY)
    dma = pltpu.SemaphoreType.DMA
    out_shape = (
        shape((tokens, d_model), BF16),
        shape((d_blk, d_ff), F32),
        shape((d_ff // 8, d_model), F32),
        shape((8, d_blk, d_ff), BF16),
        shape((d_ff, d_model), BF16),
        shape((tokens, d_model), BF16),
        shape((tokens, d_model), BF16),
        shape((tokens, d_ff), BF16),
        shape((d_ff, tokens), BF16),
        shape((tokens, d_ff), BF16),
        shape((d_ff, tokens), BF16),
        shape((N_PRE, tokens, fc), BF16),
        shape((N_PRE, tokens - tokens // 3, fc), BF16),
        shape((N_FOUR, 4) + blk, F32),
        shape((N_FOUR, 2) + blk, F32),
        shape((N_FOUR,) + blk, F32),
        shape((N_FOUR, 2) + blk, F32),
        shape((N_FOUR, 2) + blk, F32),
        shape((N_FOUR,) + blk, F32),
        shape((N_PAIR, 2) + blk, F32),
        shape((N_PAIR,) + blk, F32),
    )
    outs = pl.pallas_call(
        functools.partial(kernel, (tokens, d_model, d_ff)),
        out_shape=out_shape,
        in_specs=[any_spec] * 4,
        out_specs=tuple([any_spec] * len(out_shape)),
        scratch_shapes=[
            pltpu.VMEM((tokens, d_model), BF16),
            pltpu.VMEM((tokens, d_model), BF16),
            pltpu.VMEM((tokens, d_model), BF16),
            pltpu.VMEM((tokens, d_model), BF16),
            pltpu.VMEM((tokens, d_model), F32),
            dma((7, 4)), dma((7, 4)), dma((7, 4)), dma((7, 4)), dma((6,)), dma((6,)),
            dma((2, N_FOUR)), dma((3, N_FOUR)), dma((2,)), dma((N_H,)), dma((N_PAIR,)), dma((N_PAIR,)),
            dma((4,)), dma((4,)), dma((4,)),
        ],
        compiler_params=pltpu.CompilerParams(collective_id=0, has_side_effects=True, vmem_limit_bytes=67000000),
        name="mlp_step",
    )(w1, w2, x, g)
    return deliver(outs[0], outs[1], outs[2])


N_PART = 4


def deliver(y, gup, gdown):
    def body(y_in, up_in, down_in, y_out, up_out, down_out, y_buf, up_buf, down_buf, sems_in, sems_out):
        srcs, dsts, bufs = (y_in, up_in, down_in), (y_out, up_out, down_out), (y_buf, up_buf, down_buf)
        moves = []
        for p in range(N_PART):
            for n in range(3):
                rows = srcs[n].shape[0] // N_PART
                part = pl.ds(p * rows, rows)
                moves.append((pltpu.make_async_copy(srcs[n].at[part, :], bufs[n].at[part, :], sems_in.at[n, p]),
                              pltpu.make_async_copy(bufs[n].at[part, :], dsts[n].at[part, :], sems_out.at[n, p])))
        for cp, _ in moves:
            cp.start()
        for cp_in, cp_out in moves:
            cp_in.wait()
            cp_out.start()
        for _, cp in moves:
            cp.wait()

    any_spec = pl.BlockSpec(memory_space=pl.ANY)
    arrays = (y, gup, gdown)
    return pl.pallas_call(
        body,
        out_shape=tuple(jax.ShapeDtypeStruct(a.shape, a.dtype) for a in arrays),
        in_specs=[any_spec] * 3,
        out_specs=(any_spec,) * 3,
        scratch_shapes=[pltpu.VMEM(a.shape, a.dtype) for a in arrays] +
        [pltpu.SemaphoreType.DMA((3, N_PART)), pltpu.SemaphoreType.DMA((3, N_PART))],
        compiler_params=pltpu.CompilerParams(vmem_limit_bytes=60000000),
        name="deliver",
    )(*arrays)


def solution(mesh):
    row_spec = P(None, 'fsdp', None)

    def per_device(w_up, w_down, tokens_in, cotangent):
        width = tokens_in.shape[-1]
        y, gup, gdown = fused_step(w_up[0], w_down[0], tokens_in.reshape(-1, width), cotangent.reshape(-1, width))
        return y.reshape(tokens_in.shape), gup[None], gdown[None]

    return jax.shard_map(per_device, mesh=mesh, in_specs=(row_spec,) * 4, out_specs=(row_spec,) * 3, check_vma=False)
```

time: 2380 us -> 550 us (0.23)
  waiting for transfers between devices: 1990 us -> 0 us
  Pallas kernels: 0 us -> 548 us
  matrix products: 322 us -> 0 us
  other arithmetic: 45.6 us -> 0 us
    reduce_scatter x6 -> x0, waiting for transfers between devices: 1370 us -> none  [the longest x3 755 us: micro_step(): lax.psum_scatter(part_down, 'fsdp', scatter_dimension=0, tiled=True)]
    all_gather x6 -> x0, waiting for transfers between devices: 620 us -> none  [the longest x3 339 us: gather_layer(): full_up = lax.all_gather(up_shard, 'fsdp', axis=0, tiled=True)]
    pallas_call x0 -> x2, Pallas kernels: none -> 548 us  [the longest x1 535 us: fused_step(): pl.pallas_call(functools.partial(kernel, (tokens, d_model, d_ff)), out_sh...]
    dot_general x12 -> x0, matrix products: 322 us -> none  [the longest x3 116 us: micro_step(): jnp.einsum('td,tf->df', rows_prev, grad_pre, preferred_element_type=jnp.f...]
    add x6 -> x0, other arithmetic: 45.6 us -> none  [the longest x3 24.3 us: micro_step(): acc_down[layer_idx]]
  transfers between devices with their start and end apart: 12 -> 0, of which waited for: 12 -> 0; matrix products, arithmetic and copies ran while one was open for 10% -> 0% of each run, Pallas kernels for 0% -> 0%
where the time goes in v3:
time: 550 us; the launch traced here: 549 us
  Pallas kernels  548 us (100%)
    pallas_call x1, Pallas kernels, fused_step(): pl.pallas_call(functools.partial(kernel, (tokens, d_model, d_ff)), out_sh...  535 us
    pallas_call x1, Pallas kernels, deliver(): pl.pallas_call(body, out_shape=tuple((jax.ShapeDtypeStruct(a.shape, a.dty...  12.8 us

profile of v3, /device:TPU:0, one launch (start us, length us, event | category | flops | bytes accessed | tf_op | source)
XLA Modules:
  0.0 548.7 jit_solution(1648029200366299654)
XLA Ops:
  0.6 535.0 %mlp_step.1 = (bf16[1536,2048]{1,0:T(8,128)(2,1)}, f32[256,5632]{1,0:T(8,128)}, f32[704,2048]{1,0:T(8,128)}, bf16[8,256,5632]{2,1,0:T(8,128)(2,1)}, bf16[5632,20...) custom-call(bf16[256,5632]{1,0:T(8,128)(2,1)} %bitcast.9, ...), custom_call_target="tpu_custom_call" | custom-call | tf_op jit(solution)/shard_map/mlp_step/pallas_call | solution.py:819
  535.7 12.8 %deliver.1 = (bf16[1536,2048]{1,0:T(8,128)(2,1)}, f32[256,5632]{1,0:T(8,128)}, f32[704,2048]{1,0:T(8,128)}) custom-call(bf16[1536,2048]{1,0:T(8,128)(2,1)} %get-tuple-element.9.y_in, f32[256,5632]{1,0:T(8,128)} %get-tuple-element.10.up_in, f32[704,2048]{1,0:T(8,128)} %get-tuple-element.11.down_in), custom_call_target="tpu_custom_call" | custom-call | tf_op jit(solution)/shard_map/deliver/pallas_call | solution.py:863

commit v4 on v3

--- a/solution.py
+++ b/solution.py
@@ -19,7 +19,7 @@
 N_K = 5
 N_H = 6
 N_SPLIT = 8
-T_STEP = 11
+T_STEP = 10
 GELU_C = math.sqrt(2.0 / math.pi)
 NN = (((1,), (0,)), ((), ()))
 NT = (((1,), (1,)), ((), ()))
@@ -837,7 +837,7 @@
     return deliver(outs[0], outs[1], outs[2])
 
 
-N_PART = 4
+N_PART = 8
 
 
 def deliver(y, gup, gdown):

time: 550 us -> 550 us (level)
  no operation moved by 1% of the time
where the time goes in v4:
time: 550 us; the launch traced here: 549 us
  Pallas kernels  548 us (100%)
    pallas_call x1, Pallas kernels, fused_step(): pl.pallas_call(functools.partial(kernel, (tokens, d_model, d_ff)), out_sh...  535 us
    pallas_call x1, Pallas kernels, deliver(): pl.pallas_call(body, out_shape=tuple((jax.ShapeDtypeStruct(a.shape, a.dty...  12.8 us

profile of v4, /device:TPU:0, one launch (start us, length us, event | category | flops | bytes accessed | tf_op | source)
XLA Modules:
  0.0 548.6 jit_solution(14572765780175803392)
XLA Ops:
  0.6 535.0 %mlp_step.1 = (bf16[1536,2048]{1,0:T(8,128)(2,1)}, f32[256,5632]{1,0:T(8,128)}, f32[704,2048]{1,0:T(8,128)}, bf16[8,256,5632]{2,1,0:T(8,128)(2,1)}, bf16[5632,20...) custom-call(bf16[256,5632]{1,0:T(8,128)(2,1)} %bitcast.9, ...), custom_call_target="tpu_custom_call" | custom-call | tf_op jit(solution)/shard_map/mlp_step/pallas_call | solution.py:819
  535.7 12.8 %deliver.1 = (bf16[1536,2048]{1,0:T(8,128)(2,1)}, f32[256,5632]{1,0:T(8,128)}, f32[704,2048]{1,0:T(8,128)}) custom-call(bf16[1536,2048]{1,0:T(8,128)(2,1)} %get-tuple-element.9.y_in, f32[256,5632]{1,0:T(8,128)} %get-tuple-element.10.up_in, f32[704,2048]{1,0:T(8,128)} %get-tuple-element.11.down_in), custom_call_target="tpu_custom_call" | custom-call | tf_op jit(solution)/shard_map/deliver/pallas_call | solution.py:863
